TPU v7x, 32 devices: a whole 2x2x4 slice. The times are simulated.
32 devices in a mesh: sfc: 16 (over z, y, x), grp: 2 (over core).
Axes of the slice: x: 2, y: 2, z: 4, core: 2. Of those that a mesh axis runs over, the one named last changes fastest.
Arguments:
- right_side: float32 [5, 5, 5, 4096], P(None, None, None, ('sfc', 'grp')), may hold values from -8 to 8
- cell_level: int32 [4096], P(('sfc', 'grp')), may hold values from 0 to 3
- own_slot: int32 [12288], P(('sfc', 'grp')), may hold values from 0 to 767
- near_slot: int32 [12288], P(('sfc', 'grp')), may hold values from 0 to 1151, as said below
- face_kind: int32 [12288], P(('sfc', 'grp')), may hold values from 0 to 5
- orientation: int32 [12288], P(('sfc', 'grp')), may hold values from 0 to 7
- penalty: float32 [12288], P(('sfc', 'grp')), may hold values from 2 to 32
- send_slots: int32 [12288], P(('sfc', 'grp')), may hold values from 0 to 767
- subface_maps: float32 [4, 25, 25], replicated, may hold values from -1.25 to 1.25
Outputs:
- solution: float32 [5, 5, 5, 4096], P(None, None, None, ('sfc', 'grp'))
- residual: float32 [5, 5, 5, 4096], P(None, None, None, ('sfc', 'grp'))
Inputs may be any that keep to these rules, and one draw needn't show every extreme that they name: `own_slot`: a face slot f * 128 + c of the same device. `near_slot`: 768 + k * 96 + i for position i of the received block k; since a device has exactly 384 entries, its near slots are a permutation of its 384 received positions. `face_kind`: 0 boundary face, 1 conforming face, 2 + s the fine side of a hanging face with subface s. `send_slots`: a device's entries k * 96 to k * 96 + 95 are face slots of its own cells sent to the device at offset (+1, -1, +2, -2)[k].
All inputs are finite; a program needn't handle non-finite values.
Results may differ from a plain program's by a relative error of at most 0.00021.
Values sent between devices are 32-bit elements; how exact they have to be, the bound alone decides.
A program may use at most 64 MiB of HBM per device.

v0:
```python
import functools

import jax
import jax.numpy as jnp
import numpy as np
from jax import lax
from jax.experimental import pallas as pl
from jax.experimental.pallas import tpu as pltpu
from jax.sharding import PartitionSpec as P

NODES = 5
WIDTH = NODES * NODES
ROWS = 32
CUBE = 128
ITERS = 3
OFFSETS = (1, -1, 2, -2)
MASS = 1.0
MESH = pl.DeviceIdType.MESH
F32 = jnp.float32
BF16 = jnp.bfloat16


def node_tables():
    points = np.array([-1.0, -np.sqrt(3.0 / 7.0), 0.0, np.sqrt(3.0 / 7.0), 1.0])
    weights = np.array([0.1, 49.0 / 90.0, 32.0 / 45.0, 49.0 / 90.0, 0.1])
    identity = np.eye(5)
    spacing = points[:, None] - points[None, :] + identity
    barycentric = 1.0 / np.prod(spacing, axis=1)
    offdiag = barycentric[None, :] / barycentric[:, None] / spacing
    diagonal = np.sum(1.0 / spacing, axis=1) - 1.0
    derivs = np.where(identity > 0.5, diagonal[:, None], offdiag)
    return derivs.T @ (weights[:, None] * derivs), weights


def constants():
    stiff, w = node_tables()
    mass = np.diag(w)
    kron = lambda a, b, c: np.kron(np.kron(a, b), c)
    volume = np.zeros((CUBE, CUBE))
    volume[:125, :125] = kron(stiff, mass, mass) + kron(mass, stiff, mass) + kron(mass, mass, stiff)
    high = volume.astype(jnp.bfloat16)
    low = (volume - high.astype(np.float64)).astype(jnp.bfloat16)
    volume = np.concatenate([high, high, low], axis=1)
    nodes = np.arange(125).reshape(5, 5, 5)
    layers = [nodes[0], nodes[4], nodes[:, 0], nodes[:, 4], nodes[:, :, 0], nodes[:, :, 4]]
    select = np.zeros((6 * ROWS, CUBE))
    for face, layer in enumerate(layers):
        select[face * ROWS + np.arange(WIDTH), layer.reshape(-1)] = 1.0
    lift = np.concatenate([select.T, select.T], axis=1)
    turn = np.zeros((8, ROWS, ROWS))
    for code in range(8):
        order = np.arange(WIDTH).reshape(5, 5)
        order = order[::-1] if code & 1 else order
        order = order[:, ::-1] if code & 2 else order
        order = order.T if code & 4 else order
        turn[code, np.arange(WIDTH), order.reshape(-1)] = 1.0
    back = np.swapaxes(turn, 1, 2)
    turns = [np.concatenate([m, m], axis=2).reshape(8 * ROWS, 2 * ROWS) for m in (turn, back)]
    face_mass = np.zeros((ROWS, 128))
    face_mass[:WIDTH] = np.outer(w, w).reshape(-1, 1)
    cube_mass = np.zeros((CUBE, 128))
    cube_mass[:125] = MASS * np.einsum("a,b,c->abc", w, w, w).reshape(-1, 1)
    bf = lambda a: jnp.asarray(np.asarray(a, np.float32), BF16)
    return (
        bf(volume),
        bf(select),
        bf(lift),
        bf(turns[0]),
        bf(turns[1]),
        jnp.asarray(np.concatenate([face_mass, cube_mass]), F32),
    )


def split(x):
    high = x.astype(BF16)
    return high, (x - high.astype(F32)).astype(BF16)


def dot(a, b):
    return jnp.dot(a, b, preferred_element_type=F32)


def dot_nt(a, b):
    return lax.dot_general(a, b, (((1,), (1,)), ((), ())), preferred_element_type=F32)


def ring_levels(total):
    levels, stride = [], 1
    while stride < total:
        rest = total // stride
        size = max(g for g in range(1, 33) if rest % g == 0)
        size = rest if size == 1 else size
        levels.append((stride, size))
        stride *= size
    return levels


def tail_rows(ghost, pad):
    return ROWS // 2 if pad == 128 and 64 < ghost <= 96 else ROWS


def pack(first, second, ghost, pad):
    if tail_rows(ghost, pad) == ROWS:
        return first, second
    lane = lax.broadcasted_iota(jnp.int32, (ROWS, pad), 1)
    half = ROWS // 2
    moved = pltpu.roll(second, ghost, 1)
    tail = jnp.where(lane[:half] < 64, moved[:half], pltpu.roll(moved[half:], 64, 1))
    return jnp.where(lane < ghost, first, moved), tail


def unpack(main, tail, ghost, pad):
    if tail_rows(ghost, pad) == ROWS:
        return main, tail
    lane = lax.broadcasted_iota(jnp.int32, (ROWS, pad), 1)
    moved = jnp.concatenate([tail, pltpu.roll(tail, 64, 1)], axis=0)
    return main, pltpu.roll(jnp.where(lane < ghost, moved, main), pad - ghost, 1)


def kernel(
    dims,
    rhs_ref, level_ref, own_ref, near_ref, kind_ref, orient_ref, pen_ref, send_ref, maps_ref,
    vol_ref, sel_ref, lift_ref, turn_ref, back_ref, mass_ref,
    x_out, r_out,
    field, gather, mapz, diag, psrc, pbuf, xsrc, xbuf, asrc, *rest,
):
    n_sfc, n_grp, count, ghost, pad = dims
    total = n_sfc * n_grp
    levels = ring_levels(total)
    slots_refs = rest[: len(levels)]
    psend, precv, xsend, xrecv, asend, arecv = rest[len(levels):]
    me = lax.axis_index("sfc") * n_grp + lax.axis_index("grp")
    slots = 6 * count
    entries = 4 * ghost
    cols = 4 * pad

    def place(device):
        return (device // n_grp, lax.rem(device, n_grp))

    def near_device(k):
        return place(lax.rem(me + OFFSETS[k] + total, total))

    def peer(level, step):
        stride, size = levels[level]
        digit = lax.rem(me // stride, size)
        return place(me + (lax.rem(digit + step, size) - digit) * stride)

    exists = [(me + offset >= 0) & (me + offset < total) for offset in OFFSETS]

    def guarded(k, action):
        @pl.when(exists[k])
        def _():
            action()

    for k in range(4):
        @pl.when(jnp.logical_not(exists[k]))
        def _(k=k):
            pbuf[k] = jnp.zeros((8, pad), F32)
            for it in range(ITERS):
                xbuf[it, k] = jnp.zeros(xbuf.shape[2:], F32)

    barrier = pltpu.get_barrier_semaphore()
    greeted = 0
    for level, (_, size) in enumerate(levels):
        def greet(step, carry, level=level):
            pl.semaphore_signal(barrier, inc=1, device_id=peer(level, step), device_id_type=MESH)
            return carry
        lax.fori_loop(1, size, greet, 0)
        greeted += size - 1
    if len(levels) > 1:
        for k in range(4):
            pl.semaphore_signal(barrier, inc=1, device_id=near_device(k), device_id_type=MESH)
        greeted += 4

    line = lambda ref: ref[...].reshape(1, -1)
    own = line(own_ref)
    high_slot = (own >> 8).astype(F32)
    low_slot = (own & 255).astype(F32)
    pen = line(pen_ref)
    pen_a = pen.astype(BF16).astype(F32)
    pen_b = (pen - pen_a).astype(BF16).astype(F32)
    pen_c = pen - pen_a - pen_b
    send = line(send_ref)
    zero_row = jnp.zeros_like(pen)
    params = jnp.concatenate(
        [high_slot, low_slot, line(kind_ref).astype(F32), line(orient_ref).astype(F32), pen_a, pen_b, pen_c, zero_row],
        axis=0,
    ).astype(BF16)
    sent_rows = jnp.concatenate(
        [(send >> 8).astype(F32), (send & 255).astype(F32)] + [zero_row] * 6, axis=0
    ).astype(BF16)
    near = jnp.broadcast_to(line(near_ref), (pad, entries))
    spot = lax.broadcasted_iota(jnp.int32, (pad, entries), 0)
    lane = lax.broadcasted_iota(jnp.int32, (pad, entries), 1)
    inside = spot < ghost
    order, spread = [], []
    for k in range(4):
        order.append(jnp.where(inside & (near == spot + (slots + k * ghost)), 1.0, 0.0).astype(BF16))
        spread.append(jnp.where(inside & (lane == spot + k * ghost), 1.0, 0.0).astype(BF16))
    ordered = dot_nt(params, jnp.concatenate(order, axis=0))
    spread = dot_nt(sent_rows, jnp.concatenate(spread, axis=0))
    own_slot = (ordered[0:1] * 256.0 + ordered[1:2]).astype(jnp.int32)
    send_slot = (spread[0:1] * 256.0 + spread[1:2]).astype(jnp.int32)
    slot_row = lax.broadcasted_iota(jnp.int32, (slots, cols), 0)
    gather[:, cols:] = jnp.where(slot_row == own_slot, 1.0, 0.0).astype(BF16)
    scale = jnp.exp2(-line(level_ref).astype(F32))
    scale_all = jnp.concatenate([jnp.broadcast_to(scale, (8, count))] * 6, axis=1).astype(BF16)
    own_scale = dot(scale_all, gather[:, cols:])[0:1]
    strength = (ordered[4:5] + ordered[5:6] + ordered[6:7]) * own_scale
    sub = lax.broadcasted_iota(jnp.int32, (8, cols), 0)
    tile = jnp.where(sub == 0, ordered[2:3], jnp.where(sub == 1, ordered[3:4], jnp.where(sub == 2, strength, 0.0)))
    for k in range(4):
        psrc[k] = tile[:, k * pad : (k + 1) * pad]

    pl.semaphore_wait(barrier, greeted)

    pcopies = []
    for k in range(4):
        pcopies.append(pltpu.make_async_remote_copy(
            src_ref=psrc.at[k], dst_ref=pbuf.at[k], send_sem=psend.at[k], recv_sem=precv.at[k],
            device_id=near_device(k ^ 1), device_id_type=MESH,
        ))
        guarded(k ^ 1, pcopies[-1].start)

    gather[:, :cols] = jnp.where(slot_row == send_slot, 1.0, 0.0).astype(BF16)
    mapz[...] = jnp.zeros_like(mapz)
    for s in range(4):
        mapz[s * ROWS : s * ROWS + WIDTH, 0:WIDTH] = maps_ref[:, s, :]
    maps = mapz[...]
    map_high, map_low = split(maps[:, :ROWS])
    back_high, back_low = split(maps.T[:ROWS])
    back_twice = jnp.concatenate([back_high, back_high], axis=1)
    face_mass = jnp.concatenate([mass_ref[:ROWS]] * (cols // 128), axis=1)
    cube_mass = mass_ref[ROWS:]
    mass_scale = cube_mass * (scale * scale * scale)
    field[...] = jnp.zeros_like(field)
    for g in range(WIDTH):
        field[g * NODES : (g + 1) * NODES] = rhs_ref[g]
    right = field[...]

    def traces(v_high, v_low):
        both = dot(sel_ref[...], jnp.concatenate([v_high, v_low], axis=1))
        rows = [both[f * ROWS : (f + 1) * ROWS] for f in range(6)]
        return jnp.concatenate(
            [
                jnp.concatenate([row[:, :count] for row in rows], axis=1),
                jnp.concatenate([row[:, count:] for row in rows], axis=1),
            ],
            axis=0,
        ).astype(BF16)

    near_info = []
    xcopies = []

    def turned(values, codes, table):
        high, low = split(values)
        forms = dot(table[...], jnp.concatenate([high, low], axis=0))
        result = forms[:ROWS]
        for code in range(1, 8):
            result = jnp.where(codes == code, forms[code * ROWS : (code + 1) * ROWS], result)
        return result

    def operator(v, turn_number):
        v_high, v_low = split(v)
        picked = dot(traces(v_high, v_low), gather[...])
        picked = picked[:ROWS] + picked[ROWS:]
        own_side = picked[:, cols:]
        if not near_info:
            for k in range(4):
                guarded(k, pcopies[k].wait_recv)
            info = jnp.concatenate([pbuf[k] for k in range(4)], axis=1)
            near_info.append(info[0:1].astype(jnp.int32))
            near_info.append(info[1:2].astype(jnp.int32))
            power = jnp.concatenate([pbuf[k][2:3] for k in range(4)], axis=1)
            diag[:, :cols] = face_mass * power
            diag[:, cols:] = face_mass * strength
        kinds, codes = near_info
        oriented = turned(picked[:, :cols], codes, turn_ref)
        high, low = split(oriented)
        forms = dot(map_high, high) + dot(map_high, low) + dot(map_low, high)
        near_side = jnp.where(kinds == 1, oriented, 0.0)
        for s in range(4):
            near_side = jnp.where(kinds == s + 2, forms[s * ROWS : (s + 1) * ROWS], near_side)
        for k in range(4):
            main, tail = pack(
                near_side[:, k * pad : (k + 1) * pad], own_side[:, (k ^ 1) * pad : ((k ^ 1) + 1) * pad], ghost, pad
            )
            xsrc[turn_number, k, :ROWS] = main
            xsrc[turn_number, k, ROWS:] = tail
        copies = []
        for k in range(4):
            copies.append(pltpu.make_async_remote_copy(
                src_ref=xsrc.at[turn_number, k], dst_ref=xbuf.at[turn_number, k ^ 1],
                send_sem=xsend.at[turn_number, k], recv_sem=xrecv.at[turn_number, k ^ 1],
                device_id=near_device(k), device_id_type=MESH,
            ))
        for k in (2, 3, 0, 1):
            guarded(k, copies[k].start)
        xcopies.append(copies)
        image = dot(vol_ref[:, : 2 * CUBE], jnp.concatenate([v_high, v_low], axis=0))
        image = (image + dot(vol_ref[:, 2 * CUBE :], v_high)) * scale + mass_scale * v
        for k in range(4):
            guarded(k ^ 1, copies[k].wait_recv)
        got = [unpack(xbuf[turn_number, k, :ROWS], xbuf[turn_number, k, ROWS:], ghost, pad) for k in range(4)]
        near_got = jnp.concatenate([got[k][1] for k in range(4)], axis=1)
        own_got = jnp.concatenate([got[k ^ 1][0] for k in range(4)], axis=1)
        near_flux = diag[:, :cols] * (near_side - near_got)
        own_flux = diag[:, cols:] * (own_side - own_got)
        stacked = jnp.concatenate([jnp.where(kinds == s + 2, near_flux, 0.0) for s in range(4)], axis=0)
        high, low = split(stacked)
        near_flux = jnp.where(kinds == 1, near_flux, 0.0)
        near_flux = near_flux + dot(back_twice, jnp.concatenate([high, low], axis=0)) + dot(back_low, high)
        near_flux = turned(near_flux, codes, back_ref)
        flux = jnp.concatenate([near_flux, own_flux], axis=1)
        faces = dot_nt(jnp.concatenate(split(flux), axis=0), gather[...])
        faces = faces[:ROWS] + faces[ROWS:]
        faces = jnp.concatenate([faces[:, f * count : (f + 1) * count] for f in range(6)], axis=0)
        return image + dot(lift_ref[...], jnp.concatenate(split(faces), axis=0))

    def level_copy(turn_number, level, step):
        return pltpu.make_async_remote_copy(
            src_ref=asrc.at[turn_number, level], dst_ref=slots_refs[level].at[turn_number, step - 1],
            send_sem=asend.at[turn_number, level], recv_sem=arecv.at[turn_number, level],
            device_id=peer(level, step), device_id_type=MESH,
        )

    def level_start(turn_number, level):
        def start(step, carry):
            level_copy(turn_number, level, step).start()
            return carry
        lax.fori_loop(1, levels[level][1], start, 0)

    def sums_start(turn_number, pairs):
        lane = lax.broadcasted_iota(jnp.int32, (1, 128), 1)
        row = jnp.zeros((1, 128), F32)
        for i, (a, b) in enumerate(pairs):
            part = jnp.sum(jnp.sum(a * b, axis=0, keepdims=True), axis=1, keepdims=True)
            row = jnp.where(lane == i, part, row)
        asrc[turn_number, 0] = row
        level_start(turn_number, 0)

    def sums_wait(turn_number, number):
        for level in range(len(levels)):
            landed = slots_refs[level].at[turn_number]
            pltpu.make_async_copy(landed, landed, arecv.at[turn_number, level]).wait()
            value = asrc[turn_number, level] + jnp.sum(landed[...], axis=0)
            if level + 1 < len(levels):
                asrc[turn_number, level + 1] = value
                level_start(turn_number, level + 1)
        return [value[:, i : i + 1] for i in range(number)]

    asrc[...] = jnp.zeros_like(asrc)
    r = right
    w = operator(r, 0)
    x = p = s = z = None
    norm_last = None
    for it in range(ITERS):
        pairs = [(r, r), (r, w)]
        if it:
            pairs += [(r, s), (p, w), (p, s)]
        sums_start(it, pairs)
        q = operator(w, it + 1) if it + 1 < ITERS else None
        sums = sums_wait(it, len(pairs))
        norm = sums[0]
        if it == 0:
            alpha = norm / sums[1]
            p, s, z = r, w, q
            x = alpha * p
        else:
            beta = norm / norm_last
            alpha = norm / (sums[1] + beta * (sums[2] + sums[3]) + beta * beta * sums[4])
            p = r + beta * p
            s = w + beta * s
            x = x + alpha * p
            if q is not None:
                z = q + beta * z
        r = r - alpha * s
        if q is not None:
            w = w - alpha * z
        norm_last = norm

    field[...] = x
    for g in range(WIDTH):
        x_out[g] = field[g * NODES : (g + 1) * NODES]
    mapz[...] = r
    for g in range(WIDTH):
        r_out[g] = mapz[g * NODES : (g + 1) * NODES]

    for k in range(4):
        guarded(k ^ 1, pcopies[k].wait_send)
        for copies in xcopies:
            guarded(k, copies[k].wait_send)
    for it in range(ITERS):
        for level in range(len(levels)):
            landed = slots_refs[level].at[it]
            pltpu.make_async_copy(landed, landed, asend.at[it, level]).wait()


def body(n_sfc, n_grp, right_side, cell_level, own_slot, near_slot, face_kind, orientation, penalty, send_slots, maps):
    count = right_side.shape[-1]
    ghost = send_slots.shape[0] // 4
    pad = -(-ghost // 128) * 128
    levels = ring_levels(n_sfc * n_grp)
    vmem = pl.BlockSpec(memory_space=pltpu.VMEM)
    dma = pltpu.SemaphoreType.DMA
    shape = jax.ShapeDtypeStruct((WIDTH, NODES, count), F32)
    x, r = pl.pallas_call(
        functools.partial(kernel, (n_sfc, n_grp, count, ghost, pad)),
        out_shape=(shape, shape),
        in_specs=[vmem] * 15,
        out_specs=(vmem, vmem),
        scratch_shapes=[
            pltpu.VMEM((CUBE, count), F32),
            pltpu.VMEM((6 * count, 8 * pad), BF16),
            pltpu.VMEM((4 * ROWS, 128), F32),
            pltpu.VMEM((ROWS, 8 * pad), F32),
            pltpu.VMEM((4, 8, pad), F32),
            pltpu.VMEM((4, 8, pad), F32),
            pltpu.VMEM((ITERS, 4, ROWS + tail_rows(ghost, pad), pad), F32),
            pltpu.VMEM((ITERS, 4, ROWS + tail_rows(ghost, pad), pad), F32),
            pltpu.VMEM((ITERS, len(levels), 1, 128), F32),
        ]
        + [pltpu.VMEM((ITERS, size - 1, 1, 128), F32) for _, size in levels]
        + [
            dma((4,)),
            dma((4,)),
            dma((ITERS, 4)),
            dma((ITERS, 4)),
            dma((ITERS, len(levels))),
            dma((ITERS, len(levels))),
        ],
        compiler_params=pltpu.CompilerParams(collective_id=0, has_side_effects=True),
    )(
        right_side.reshape(WIDTH, NODES, count),
        cell_level, own_slot, near_slot, face_kind, orientation, penalty, send_slots,
        jnp.swapaxes(maps, 0, 1), *constants(),
    )
    return x.reshape(right_side.shape), r.reshape(right_side.shape)


def solution(mesh):
    split_spec = P(("sfc", "grp"))
    field_spec = P(None, None, None, ("sfc", "grp"))
    return jax.shard_map(
        functools.partial(body, mesh.shape["sfc"], mesh.shape["grp"]),
        mesh=mesh,
        in_specs=(field_spec,) + (split_spec,) * 7 + (P(),),
        out_specs=(field_spec, field_spec),
        check_vma=False,
    )
```

profile of v0, /device:TPU:0, one launch (start us, length us, event | category | flops | bytes accessed | tf_op | source)
XLA Modules:
  0.0 38.4 jit_solution(4424516908528499568)
XLA Ops:
  0.6 35.5 %shard_map.158 = (f32[25,5,128]{2,1,0:T(8,128)}, f32[25,5,128]{2,1,0:T(8,128)}) custom-call(f32[25,5,128]{2,1,0:T(8,128)} %bitcast.6, s32[128]{0:T(128)} %level_ref.1, s32[384]{0:T(512)} %own_ref.1, s32[384]{0:T(512)} %near_ref.1, s32[384]{0:T(512)} %kind_ref.1, s32[384]{0:T(512)} %orient_ref.1, f32[384]{0:T(512)} %pen_ref.1, s32[384]{0:T(512)} %send_ref.1, ...), custom_call_target="tpu_custom_call" | custom-call | tf_op jit(solution)/shard_map/pallas_call | solution.py:407
  36.1 0.0 copy-start
  36.2 1.6 %copy.19 = f32[5,5,5,128]{3,2,1,0:T(8,128)} copy(f32[5,5,5,128]{3,2,1,0:T(8,128)} %bitcast.5) | data formatting | bytes 128000
  37.7 0.0 copy-done
  37.7 0.6 %copy.20 = f32[5,5,5,128]{3,2,1,0:T(8,128)} copy(f32[5,5,5,128]{3,2,1,0:T(8,128)S(1)} %bitcast.4) | data formatting | bytes 128000
Async XLA Ops:
  36.1 1.6 %copy-start = (f32[25,5,128]{2,1,0:T(8,128)S(1)}, f32[25,5,128]{2,1,0:T(8,128)}, u32[]{:S(2)}) copy-start(f32[25,5,128]{2,1,0:T(8,128)} %get-tuple-element.5) | copy-start | bytes 192004
where the time goes:
time: 38.6 us; the launch traced here: 38.4 us
  Pallas kernels  35.5 us (92%)
  local copies, waits for them, and re-layouts  2.22 us (6%)
  between operations  0.65 us (2%)
    pallas_call x1, Pallas kernels, body(): pl.pallas_call(functools.partial(kernel, (n_sfc, n_grp, count, ghost, pad...  35.5 us
    unnamed x4, local copies, waits for them, and re-layouts  2.22 us

commit v1 on v0

v1 whole, which is shorter than its diff:
```python
import functools

import jax
import jax.numpy as jnp
import numpy as np
from jax import lax
from jax.experimental import pallas as pl
from jax.experimental.pallas import tpu as pltpu
from jax.sharding import PartitionSpec as P

NODES = 5
WIDTH = NODES * NODES
ROWS = 32
FACES = 6 * ROWS
CUBE = 208
ITERS = 3
MOMENTS = 2 * ITERS
MESSAGE = 56
UNIT = 2.0**-12
OFFSETS = (1, -1, 2, -2)
MASS = 1.0
MESH = pl.DeviceIdType.MESH
F32 = jnp.float32
BF16 = jnp.bfloat16


def node_tables():
    points = np.array([-1.0, -np.sqrt(3.0 / 7.0), 0.0, np.sqrt(3.0 / 7.0), 1.0])
    weights = np.array([0.1, 49.0 / 90.0, 32.0 / 45.0, 49.0 / 90.0, 0.1])
    identity = np.eye(5)
    spacing = points[:, None] - points[None, :] + identity
    barycentric = 1.0 / np.prod(spacing, axis=1)
    offdiag = barycentric[None, :] / barycentric[:, None] / spacing
    diagonal = np.sum(1.0 / spacing, axis=1) - 1.0
    derivs = np.where(identity > 0.5, diagonal[:, None], offdiag)
    return derivs.T @ (weights[:, None] * derivs), weights


def constants():
    stiff, w = node_tables()
    mass = np.diag(w)
    kron = lambda a, b, c: np.kron(np.kron(a, b), c)
    spots = (np.arange(WIDTH)[:, None] * 8 + np.arange(NODES)).reshape(-1)
    nodes = spots.reshape(5, 5, 5)
    layers = [nodes[0], nodes[4], nodes[:, 0], nodes[:, 4], nodes[:, :, 0], nodes[:, :, 4]]
    select = np.zeros((FACES, CUBE))
    for face, layer in enumerate(layers):
        select[face * ROWS + np.arange(WIDTH), layer.reshape(-1)] = 1.0
    both = np.concatenate([select, np.eye(CUBE)])
    volume = np.zeros((CUBE, CUBE))
    volume[np.ix_(spots, spots)] = kron(stiff, mass, mass) + kron(mass, stiff, mass) + kron(mass, mass, stiff)
    volume = both @ volume * UNIT
    high = volume.astype(jnp.bfloat16)
    low = (volume - high.astype(np.float64)).astype(jnp.bfloat16)
    volume = np.concatenate([high, high, low], axis=1)
    lift = both @ select.T
    lift = np.concatenate([lift, lift], axis=1)
    turn = np.zeros((8, ROWS, ROWS))
    for code in range(8):
        order = np.arange(WIDTH).reshape(5, 5)
        order = order[::-1] if code & 1 else order
        order = order[:, ::-1] if code & 2 else order
        order = order.T if code & 4 else order
        turn[code, np.arange(WIDTH), order.reshape(-1)] = 1.0
    back = np.swapaxes(turn, 1, 2)
    turns = np.concatenate([np.concatenate([m, m], axis=2).reshape(8 * ROWS, 2 * ROWS) for m in (turn, back)])
    face_mass = np.zeros((ROWS, 128))
    face_mass[:WIDTH] = UNIT * np.outer(w, w).reshape(-1, 1)
    cube_mass = np.zeros((CUBE, 128))
    cube_mass[spots] = UNIT * MASS * np.einsum("a,b,c->abc", w, w, w).reshape(-1, 1)
    bf = lambda a: jnp.asarray(np.asarray(a, np.float32), BF16)
    return (
        bf(select),
        bf(turns),
        jnp.asarray(np.concatenate([face_mass, both @ cube_mass]), F32),
        bf(volume),
        bf(lift),
    )


def high_low(x):
    high = x.astype(BF16).astype(F32)
    return high, x - high


def split(x):
    high = x.astype(BF16)
    return high, (x - high.astype(F32)).astype(BF16)


def dot(a, b):
    return jnp.dot(a, b, preferred_element_type=F32)


def dot_nt(a, b):
    return lax.dot_general(a, b, (((1,), (1,)), ((), ())), preferred_element_type=F32)


def ring_levels(total):
    levels, stride = [], 1
    while stride < total:
        rest = total // stride
        size = max(g for g in range(1, 33) if rest % g == 0)
        size = rest if size == 1 else size
        levels.append((stride, size))
        stride *= size
    return levels


def conjugate(m):
    def inner(a, b, shift):
        total = None
        for power in range(len(a) + len(b) - 1):
            weight = sum(a[i] * b[power - i] for i in range(len(a)) if 0 <= power - i < len(b))
            term = weight * m[power + shift]
            total = term if total is None else total + term
        return total

    one = jnp.ones_like(m[0])
    x, r, p = [], [one], [one]
    norm = m[0]
    for it in range(ITERS):
        alpha = norm / inner(p, p, 1)
        x = [(x[i] if i < len(x) else 0.0) + alpha * p[i] for i in range(len(p))]
        r = [one] + [-value for value in x]
        if it + 1 < ITERS:
            new = inner(r, r, 0)
            beta = new / norm
            p = [r[i] + (beta * p[i] if i < len(p) else 0.0) for i in range(len(r))]
            norm = new
    return x


def kernel(
    dims,
    rhs_hbm, level_hbm, own_hbm, near_hbm, kind_hbm, orient_hbm, pen_hbm, send_hbm, maps_hbm,
    sel_hbm, turn_hbm, mass_hbm, vol_hbm, lift_hbm,
    x_out, r_out,
    rhs_ref, level_ref, own_ref, near_ref, kind_ref, orient_ref, pen_ref, send_ref, maps_ref,
    sel_ref, turn_ref, mass_ref, vol_ref, lift_ref,
    cells, cells_t, marks, mapz, diag, xsrc, xbuf, asrc, *rest,
):
    n_sfc, n_grp, count, ghost, pad = dims
    total = n_sfc * n_grp
    levels = ring_levels(total)
    slots_refs = rest[: len(levels)]
    insem, xsend, xrecv, asend, arecv = rest[len(levels):]
    me = lax.axis_index("sfc") * n_grp + lax.axis_index("grp")
    slots = 6 * count
    entries = 4 * ghost
    cols = 4 * pad

    loads = {}
    for i, (name, src, dst) in enumerate([
        ("near", near_hbm, near_ref), ("own", own_hbm, own_ref), ("send", send_hbm, send_ref),
        ("level", level_hbm, level_ref), ("rhs", rhs_hbm, rhs_ref), ("sel", sel_hbm, sel_ref),
        ("kind", kind_hbm, kind_ref), ("orient", orient_hbm, orient_ref), ("pen", pen_hbm, pen_ref),
        ("turn", turn_hbm, turn_ref), ("mass", mass_hbm, mass_ref), ("maps", maps_hbm, maps_ref),
        ("vol", vol_hbm, vol_ref), ("lift", lift_hbm, lift_ref),
    ]):
        loads[name] = pltpu.make_async_copy(src, dst, insem.at[i])
        loads[name].start()

    def place(device):
        return (device // n_grp, lax.rem(device, n_grp))

    def near_device(k):
        return place(lax.rem(me + OFFSETS[k] + total, total))

    def peer(level, step):
        stride, size = levels[level]
        digit = lax.rem(me // stride, size)
        return place(me + (lax.rem(digit + step, size) - digit) * stride)

    exists = [(me + offset >= 0) & (me + offset < total) for offset in OFFSETS]

    def guarded(k, action):
        @pl.when(exists[k])
        def _():
            action()

    barrier = pltpu.get_barrier_semaphore()
    greeted = 0
    for level, (_, size) in enumerate(levels):
        def greet(step, carry, level=level):
            pl.semaphore_signal(barrier, inc=1, device_id=peer(level, step), device_id_type=MESH)
            return carry
        lax.fori_loop(1, size, greet, 0)
        greeted += size - 1
    if len(levels) > 1:
        for k in range(4):
            pl.semaphore_signal(barrier, inc=1, device_id=near_device(k), device_id_type=MESH)
        greeted += 4

    for k in range(4):
        @pl.when(jnp.logical_not(exists[k]))
        def _(k=k):
            for it in range(ITERS):
                xbuf[it, k] = jnp.zeros(xbuf.shape[2:], F32)

    for name in ("near", "own", "send", "level", "rhs", "sel", "kind", "orient", "pen"):
        loads[name].wait()
    line = lambda ref: ref[...].reshape(1, -1)

    inner = lax.broadcasted_iota(jnp.int32, (WIDTH, 8, count), 1) < NODES
    padded = jnp.concatenate([rhs_ref[...], jnp.zeros((WIDTH, 8 - NODES, count), F32)], axis=1)
    field = jnp.concatenate(
        [jnp.where(inner, padded, 0.0).reshape(WIDTH * 8, count), jnp.zeros((CUBE - WIDTH * 8, count), F32)], axis=0
    )
    field_high, field_low = split(field)
    picked = dot(sel_ref[...], jnp.concatenate([field_high, field_low], axis=1))
    scale = jnp.exp2(-line(level_ref).astype(F32))
    face_row = lax.rem(lax.broadcasted_iota(jnp.int32, (FACES, count), 0), ROWS)
    trace_high = jnp.where(face_row == WIDTH, scale, picked[:, :count])
    trace_low = picked[:, count:]

    own = line(own_ref)
    pen = line(pen_ref)
    pen_a, pen_b = high_low(pen)
    pen_b, pen_c = high_low(pen_b)
    send = line(send_ref)
    zero_row = jnp.zeros_like(pen)
    rows = [(own >> 8).astype(F32), (own & 255).astype(F32), line(kind_ref).astype(F32), line(orient_ref).astype(F32)]
    params = jnp.concatenate(rows + [pen_a, pen_b, pen_c, zero_row], axis=0).astype(BF16)
    sent_rows = jnp.concatenate([(send >> 8).astype(F32), (send & 255).astype(F32)] + [zero_row] * 6, axis=0).astype(BF16)
    near = jnp.broadcast_to(line(near_ref), (pad, entries))
    spot = lax.broadcasted_iota(jnp.int32, (pad, entries), 0)
    lane = lax.broadcasted_iota(jnp.int32, (pad, entries), 1)
    inside = spot < ghost
    order, spread = [], []
    for k in range(4):
        order.append(jnp.where(inside & (near == spot + (slots + k * ghost)), 1.0, 0.0).astype(BF16))
        spread.append(jnp.where(inside & (lane == spot + k * ghost), 1.0, 0.0).astype(BF16))
    ordered = dot_nt(params, jnp.concatenate(order, axis=0))
    spread = dot_nt(sent_rows, jnp.concatenate(spread, axis=0))
    slot = jnp.concatenate(
        [spread[0:1] * 256.0 + spread[1:2], ordered[0:1] * 256.0 + ordered[1:2]], axis=1
    ).astype(jnp.int32)
    face = jnp.zeros_like(slot)
    for f in range(1, 6):
        face = face + jnp.where(slot >= f * count, 1, 0)
    cell = slot - face * count
    cell_row = lax.broadcasted_iota(jnp.int32, (count, 2 * cols), 0)
    chosen = jnp.where(cell_row == cell, 1.0, 0.0)
    cells[:count] = chosen.astype(BF16)
    cells[count:] = chosen.astype(BF16)

    def gather(high, low):
        found = dot(jnp.concatenate([high, low], axis=1).astype(BF16), cells[...])
        raw = found[:ROWS]
        for f in range(1, 6):
            raw = jnp.where(face == f, found[f * ROWS : (f + 1) * ROWS], raw)
        return raw

    raw = gather(trace_high, trace_low)
    strength = (ordered[4:5] + ordered[5:6] + ordered[6:7]) * raw[WIDTH : WIDTH + 1, cols:]
    sub = lax.broadcasted_iota(jnp.int32, (8, cols), 0)
    tail = jnp.where(sub == 0, ordered[2:3], jnp.where(sub == 1, ordered[3:4], jnp.where(sub == 2, strength, 0.0)))

    pl.semaphore_wait(barrier, greeted)

    xcopies = []

    def send_out(turn_number, raw):
        count_rows = MESSAGE if turn_number == 0 else 2 * WIDTH
        copies = []
        for k in range(4):
            other = cols + (k ^ 1) * pad
            xsrc[turn_number, k, :WIDTH] = raw[:WIDTH, k * pad : (k + 1) * pad]
            xsrc[turn_number, k, WIDTH : 2 * WIDTH] = raw[:WIDTH, other : other + pad]
            if turn_number == 0:
                xsrc[turn_number, k, 2 * WIDTH :] = tail[: MESSAGE - 2 * WIDTH, other - cols : other - cols + pad]
            copies.append(pltpu.make_async_remote_copy(
                src_ref=xsrc.at[turn_number, k, pl.ds(0, count_rows)],
                dst_ref=xbuf.at[turn_number, k ^ 1, pl.ds(0, count_rows)],
                send_sem=xsend.at[turn_number, k], recv_sem=xrecv.at[turn_number, k ^ 1],
                device_id=near_device(k), device_id_type=MESH,
            ))
        for k in (2, 3, 0, 1):
            guarded(k, copies[k].start)
        xcopies.append(copies)

    send_out(0, raw)

    for name in ("turn", "mass", "maps", "vol", "lift"):
        loads[name].wait()
    for f in range(6):
        marks[f] = jnp.broadcast_to(jnp.where(face == f, 1.0, 0.0), (16, 2 * cols)).astype(BF16)
    cells_t[...] = chosen.T.astype(BF16)
    mapz[...] = jnp.zeros_like(mapz)
    for s in range(4):
        mapz[s * ROWS : s * ROWS + WIDTH, 0:WIDTH] = maps_ref[:, s, :]
    maps = mapz[...]
    transposed = maps.T
    backs = jnp.concatenate([transposed[:ROWS, s * ROWS : (s + 1) * ROWS] for s in range(4)], axis=0)

    def three(matrix):
        high, low = split(matrix)
        return jnp.concatenate([high, high, low], axis=1)

    forward = three(maps[:, :ROWS])
    backward = three(backs)
    face_mass = jnp.concatenate([mass_ref[:ROWS]] * (cols // 128), axis=1)
    diag[:, cols:] = face_mass * strength
    mass_scale = mass_ref[ROWS:] * (scale * scale * scale)

    def turned(values, codes, table):
        forms = dot(table, jnp.concatenate(split(values), axis=0))
        result = forms[:ROWS]
        for code in range(1, 8):
            result = jnp.where(codes == code, forms[code * ROWS : (code + 1) * ROWS], result)
        return result

    def mapped(values, kinds, table):
        high, low = split(values)
        forms = dot(table, jnp.concatenate([high, low, high], axis=0))
        result = jnp.where(kinds == 1, values, 0.0)
        for s in range(4):
            result = jnp.where(kinds == s + 2, forms[s * ROWS : (s + 1) * ROWS], result)
        return result

    turn_table = turn_ref[: 8 * ROWS]
    back_table = turn_ref[8 * ROWS :]
    own_kinds = ordered[2:3].astype(jnp.int32)
    own_codes = ordered[3:4].astype(jnp.int32)

    def image_of(state, high, low, first):
        flat = jnp.concatenate([high, low, high], axis=0)
        return dot(vol_ref[first:], flat) * scale + mass_scale[first:] * state

    def sum_all(a):
        return jnp.sum(jnp.sum(a, axis=0, keepdims=True), axis=1, keepdims=True)

    def level_copy(level, step):
        return pltpu.make_async_remote_copy(
            src_ref=asrc.at[level], dst_ref=slots_refs[level].at[step - 1],
            send_sem=asend.at[level], recv_sem=arecv.at[level],
            device_id=peer(level, step), device_id_type=MESH,
        )

    def level_start(level):
        def start(step, carry):
            level_copy(level, step).start()
            return carry
        lax.fori_loop(1, levels[level][1], start, 0)

    basis = [field]
    moments = [sum_all(field * field)]
    state = jnp.concatenate([trace_high + trace_low, field], axis=0)
    mine = None
    for it in range(ITERS):
        last = it + 1 == ITERS
        first = FACES if last else 0
        image = image_of(state[first:], field_high, field_low, first)
        near_raw, own_raw = raw[:, :cols], raw[:, cols:]
        if it:
            mine = mapped(turned(near_raw, near_codes, turn_table), near_kinds, forward)
        for k in range(4):
            guarded(k ^ 1, xcopies[it][k].wait_recv)
        filler = jnp.zeros((ROWS - WIDTH, cols), F32)
        near_got = jnp.concatenate([xbuf[it, k ^ 1, :ROWS] for k in range(4)], axis=1)
        own_got = jnp.concatenate([xbuf[it, k, WIDTH : 2 * WIDTH] for k in range(4)], axis=1)
        own_got = jnp.concatenate([own_got, filler], axis=0)
        if it == 0:
            info = [
                jnp.concatenate([xbuf[it, k, 2 * WIDTH + i : 2 * WIDTH + i + 1] for k in range(4)], axis=1)
                for i in range(3)
            ]
            near_kinds = info[0].astype(jnp.int32)
            near_codes = info[1].astype(jnp.int32)
            diag[:, :cols] = face_mass * info[2]
            mine = mapped(turned(near_raw, near_codes, turn_table), near_kinds, forward)
        theirs = mapped(turned(near_got, own_codes, turn_table), own_kinds, forward)
        jump = own_raw - theirs
        own_flux = diag[:, cols:] * jump
        if last:
            moments.append(sum_all(field * image) + sum_all(own_flux * jump))
            lane_row = lax.broadcasted_iota(jnp.int32, (1, 128), 1)
            row = jnp.zeros((1, 128), F32)
            for i, part in enumerate(moments):
                row = jnp.where(lane_row == i, part, row)
            asrc[0] = row
            level_start(0)
        near_flux = diag[:, :cols] * (mine - own_got)
        near_flux = turned(mapped(near_flux, near_kinds, backward), near_codes, back_table)
        flux = jnp.concatenate([near_flux, own_flux], axis=1)
        parts = []
        for part in split(flux):
            for f in range(6):
                for half in range(ROWS // 16):
                    parts.append(part[half * 16 : (half + 1) * 16] * marks[f])
        faces = dot(jnp.concatenate(parts, axis=0), cells_t[...])
        faces = faces[:FACES] + faces[FACES:]
        new = image + dot(lift_ref[first:], jnp.concatenate(split(faces), axis=0))
        if last:
            basis.append(new)
            break
        state = new
        trace = state[:FACES]
        trace_high, trace_low = high_low(trace)
        raw = gather(trace_high, trace_low)
        send_out(it + 1, raw)
        field = state[FACES:]
        field_high, field_low = split(field)
        moments.append(sum_all(basis[-1] * field))
        moments.append(sum_all(field * field))
        basis.append(field)

    for level in range(len(levels)):
        landed = slots_refs[level]
        pltpu.make_async_copy(landed, landed, arecv.at[level]).wait()
        value = asrc[level] + jnp.sum(landed[...], axis=0)
        if level + 1 < len(levels):
            asrc[level + 1] = value
            level_start(level + 1)
    value = jnp.broadcast_to(value, (8, 128))
    coefs = conjugate([jnp.broadcast_to(value[:, i : i + 1], (8, count)) for i in range(MOMENTS)])
    cubes = [v[: WIDTH * 8].reshape(WIDTH, 8, count) for v in basis]
    x = coefs[0] * cubes[0]
    r = cubes[0] - coefs[0] * cubes[1]
    for i in range(1, ITERS):
        x = x + coefs[i] * cubes[i]
        r = r - coefs[i] * cubes[i + 1]
    x_out[...] = (UNIT * x)[:, :NODES]
    r_out[...] = r[:, :NODES]

    for copies in xcopies:
        for k in range(4):
            guarded(k, copies[k].wait_send)
    for level in range(len(levels)):
        landed = slots_refs[level]
        pltpu.make_async_copy(landed, landed, asend.at[level]).wait()


def body(n_sfc, n_grp, right_side, cell_level, own_slot, near_slot, face_kind, orientation, penalty, send_slots, maps):
    count = right_side.shape[-1]
    ghost = send_slots.shape[0] // 4
    pad = -(-ghost // 128) * 128
    levels = ring_levels(n_sfc * n_grp)
    dma = pltpu.SemaphoreType.DMA
    shape = jax.ShapeDtypeStruct((WIDTH, NODES, count), F32)
    operands = (
        right_side.reshape(WIDTH, NODES, count),
        cell_level, own_slot, near_slot, face_kind, orientation, penalty, send_slots,
        jnp.swapaxes(maps, 0, 1), *constants(),
    )
    vmem = pl.BlockSpec(memory_space=pltpu.VMEM)
    x, r = pl.pallas_call(
        functools.partial(kernel, (n_sfc, n_grp, count, ghost, pad)),
        out_shape=(shape, shape),
        in_specs=[pl.BlockSpec(memory_space=pltpu.HBM)] * len(operands),
        out_specs=(vmem, vmem),
        scratch_shapes=[pltpu.VMEM(operand.shape, operand.dtype) for operand in operands]
        + [
            pltpu.VMEM((2 * count, 8 * pad), BF16),
            pltpu.VMEM((8 * pad, count), BF16),
            pltpu.VMEM((6, 16, 8 * pad), BF16),
            pltpu.VMEM((4 * ROWS, 128), F32),
            pltpu.VMEM((ROWS, 8 * pad), F32),
            pltpu.VMEM((ITERS, 4, MESSAGE, pad), F32),
            pltpu.VMEM((ITERS, 4, MESSAGE, pad), F32),
            pltpu.VMEM((len(levels), 1, 128), F32),
        ]
        + [pltpu.VMEM((size - 1, 1, 128), F32) for _, size in levels]
        + [
            dma((len(operands),)),
            dma((ITERS, 4)),
            dma((ITERS, 4)),
            dma((len(levels),)),
            dma((len(levels),)),
        ],
        compiler_params=pltpu.CompilerParams(
            collective_id=0, has_side_effects=True
        ),
    )(*operands)
    return x.reshape(right_side.shape), r.reshape(right_side.shape)


def solution(mesh):
    split_spec = P(("sfc", "grp"))
    field_spec = P(None, None, None, ("sfc", "grp"))
    return jax.shard_map(
        functools.partial(body, mesh.shape["sfc"], mesh.shape["grp"]),
        mesh=mesh,
        in_specs=(field_spec,) + (split_spec,) * 7 + (P(),),
        out_specs=(field_spec, field_spec),
        check_vma=False,
    )
```

time: 38.6 us -> 29.8 us (0.77)
  Pallas kernels: 35.5 us -> 26.8 us
    pallas_call x1, Pallas kernels: 35.5 us -> 26.8 us  [body(): pl.pallas_call(functools.partial(kernel, (n_sfc, n_grp, count, ghost, pad...]
where the time goes in v1:
time: 29.8 us; the launch traced here: 29.6 us
  Pallas kernels  26.8 us (90%)
  local copies, waits for them, and re-layouts  2.22 us (7%)
  between operations  0.65 us (2%)
    pallas_call x1, Pallas kernels, body(): pl.pallas_call(functools.partial(kernel, (n_sfc, n_grp, count, ghost, pad...  26.8 us
    unnamed x4, local copies, waits for them, and re-layouts  2.22 us

profile of v1, /device:TPU:0, one launch (start us, length us, event | category | flops | bytes accessed | tf_op | source)
XLA Modules:
  0.0 29.6 jit_solution(3895390631799080141)
XLA Ops:
  0.6 26.8 %shard_map.149 = (f32[25,5,128]{2,1,0:T(8,128)}, f32[25,5,128]{2,1,0:T(8,128)}) custom-call(f32[25,5,128]{2,1,0:T(8,128)} %bitcast.6, s32[128]{0:T(128)} %level_hbm.1, s32[384]{0:T(512)} %own_hbm.1, s32[384]{0:T(512)} %near_hbm.1, s32[384]{0:T(512)} %kind_hbm.1, s32[384]{0:T(512)} %orient_hbm.1, f32[384]{0:T(512)} %pen_hbm.1, s32[384]{0:T(512)} %send_hbm.1, ...), custom_call_target="tpu_custom_call" | custom-call | tf_op jit(solution)/shard_map/pallas_call | solution.py:448
  27.4 0.0 copy-start
  27.4 1.6 %copy.18 = f32[5,5,5,128]{3,2,1,0:T(8,128)} copy(f32[5,5,5,128]{3,2,1,0:T(8,128)} %bitcast.5) | data formatting | bytes 128000
  29.0 0.0 copy-done
  29.0 0.6 %copy.19 = f32[5,5,5,128]{3,2,1,0:T(8,128)} copy(f32[5,5,5,128]{3,2,1,0:T(8,128)S(1)} %bitcast.4) | data formatting | bytes 128000
Async XLA Ops:
  27.4 1.6 %copy-start = (f32[25,5,128]{2,1,0:T(8,128)S(1)}, f32[25,5,128]{2,1,0:T(8,128)}, u32[]{:S(2)}) copy-start(f32[25,5,128]{2,1,0:T(8,128)} %get-tuple-element.5) | copy-start | bytes 192004

commit v2 on v1

--- a/solution.py
+++ b/solution.py
@@ -19,7 +19,7 @@
 UNIT = 2.0**-12
 OFFSETS = (1, -1, 2, -2)
 MASS = 1.0
-MESH = pl.DeviceIdType.MESH
+LOGICAL = pl.DeviceIdType.LOGICAL
 F32 = jnp.float32
 BF16 = jnp.bfloat16
 
@@ -52,9 +52,8 @@
     volume = both @ volume * UNIT
     high = volume.astype(jnp.bfloat16)
     low = (volume - high.astype(np.float64)).astype(jnp.bfloat16)
-    volume = np.concatenate([high, high, low], axis=1)
+    volume = np.concatenate([high, low])
     lift = both @ select.T
-    lift = np.concatenate([lift, lift], axis=1)
     turn = np.zeros((8, ROWS, ROWS))
     for code in range(8):
         order = np.arange(WIDTH).reshape(5, 5)
@@ -161,18 +160,16 @@
         loads[name] = pltpu.make_async_copy(src, dst, insem.at[i])
         loads[name].start()
 
-    def place(device):
-        return (device // n_grp, lax.rem(device, n_grp))
+    exists = [(me + offset >= 0) & (me + offset < total) for offset in OFFSETS]
 
     def near_device(k):
-        return place(lax.rem(me + OFFSETS[k] + total, total))
+        return me + jnp.where(exists[k], OFFSETS[k], 0)
+
+    digits = [lax.rem(me // stride, size) for stride, size in levels]
 
     def peer(level, step):
         stride, size = levels[level]
-        digit = lax.rem(me // stride, size)
-        return place(me + (lax.rem(digit + step, size) - digit) * stride)
-
-    exists = [(me + offset >= 0) & (me + offset < total) for offset in OFFSETS]
+        return me + jnp.where(digits[level] + step >= size, step - size, step) * stride
 
     def guarded(k, action):
         @pl.when(exists[k])
@@ -182,14 +179,12 @@
     barrier = pltpu.get_barrier_semaphore()
     greeted = 0
     for level, (_, size) in enumerate(levels):
-        def greet(step, carry, level=level):
-            pl.semaphore_signal(barrier, inc=1, device_id=peer(level, step), device_id_type=MESH)
-            return carry
-        lax.fori_loop(1, size, greet, 0)
+        for step in range(1, size):
+            pl.semaphore_signal(barrier, inc=1, device_id=peer(level, step), device_id_type=LOGICAL)
         greeted += size - 1
     if len(levels) > 1:
         for k in range(4):
-            pl.semaphore_signal(barrier, inc=1, device_id=near_device(k), device_id_type=MESH)
+            pl.semaphore_signal(barrier, inc=1, device_id=near_device(k), device_id_type=LOGICAL)
         greeted += 4
 
     for k in range(4):
@@ -274,7 +269,7 @@
                 src_ref=xsrc.at[turn_number, k, pl.ds(0, count_rows)],
                 dst_ref=xbuf.at[turn_number, k ^ 1, pl.ds(0, count_rows)],
                 send_sem=xsend.at[turn_number, k], recv_sem=xrecv.at[turn_number, k ^ 1],
-                device_id=near_device(k), device_id_type=MESH,
+                device_id=near_device(k), device_id_type=LOGICAL,
             ))
         for k in (2, 3, 0, 1):
             guarded(k, copies[k].start)
@@ -325,8 +320,9 @@
     own_codes = ordered[3:4].astype(jnp.int32)
 
     def image_of(state, high, low, first):
-        flat = jnp.concatenate([high, low, high], axis=0)
-        return dot(vol_ref[first:], flat) * scale + mass_scale[first:] * state
+        both = dot(vol_ref[first : FACES + CUBE], jnp.concatenate([high, low], axis=1))
+        both = both[:, :count] + both[:, count:] + dot(vol_ref[FACES + CUBE + first :], high)
+        return both * scale + mass_scale[first:] * state
 
     def sum_all(a):
         return jnp.sum(jnp.sum(a, axis=0, keepdims=True), axis=1, keepdims=True)
@@ -335,14 +331,12 @@
         return pltpu.make_async_remote_copy(
             src_ref=asrc.at[level], dst_ref=slots_refs[level].at[step - 1],
             send_sem=asend.at[level], recv_sem=arecv.at[level],
-            device_id=peer(level, step), device_id_type=MESH,
+            device_id=peer(level, step), device_id_type=LOGICAL,
         )
 
     def level_start(level):
-        def start(step, carry):
+        for step in range(1, levels[level][1]):
             level_copy(level, step).start()
-            return carry
-        lax.fori_loop(1, levels[level][1], start, 0)
 
     basis = [field]
     moments = [sum_all(field * field)]
@@ -391,7 +385,8 @@
                     parts.append(part[half * 16 : (half + 1) * 16] * marks[f])
         faces = dot(jnp.concatenate(parts, axis=0), cells_t[...])
         faces = faces[:FACES] + faces[FACES:]
-        new = image + dot(lift_ref[first:], jnp.concatenate(split(faces), axis=0))
+        both = dot(lift_ref[first:], jnp.concatenate(split(faces), axis=1))
+        new = image + both[:, :count] + both[:, count:]
         if last:
             basis.append(new)
             break
@@ -432,6 +427,14 @@
         pltpu.make_async_copy(landed, landed, asend.at[level]).wait()
 
 
+def store(x_ref, r_ref, x_hbm, r_hbm, sems):
+    copies = [pltpu.make_async_copy(x_ref, x_hbm, sems.at[0]), pltpu.make_async_copy(r_ref, r_hbm, sems.at[1])]
+    for copy in copies:
+        copy.start()
+    for copy in copies:
+        copy.wait()
+
+
 def body(n_sfc, n_grp, right_side, cell_level, own_slot, near_slot, face_kind, orientation, penalty, send_slots, maps):
     count = right_side.shape[-1]
     ghost = send_slots.shape[0] // 4
@@ -445,10 +448,12 @@
         jnp.swapaxes(maps, 0, 1), *constants(),
     )
     vmem = pl.BlockSpec(memory_space=pltpu.VMEM)
+    hbm = pl.BlockSpec(memory_space=pltpu.HBM)
+    operands = [pltpu.with_memory_space_constraint(operand, pltpu.HBM) for operand in operands]
     x, r = pl.pallas_call(
         functools.partial(kernel, (n_sfc, n_grp, count, ghost, pad)),
-        out_shape=(shape, shape),
-        in_specs=[pl.BlockSpec(memory_space=pltpu.HBM)] * len(operands),
+        out_shape=(pltpu.VMEM(shape.shape, F32),) * 2,
+        in_specs=[hbm] * len(operands),
         out_specs=(vmem, vmem),
         scratch_shapes=[pltpu.VMEM(operand.shape, operand.dtype) for operand in operands]
         + [
@@ -470,9 +475,17 @@
             dma((len(levels),)),
         ],
         compiler_params=pltpu.CompilerParams(
-            collective_id=0, has_side_effects=True
+            collective_id=0, has_side_effects=True, vmem_limit_bytes=16 * 1024 * 1024
         ),
     )(*operands)
+    x, r = pl.pallas_call(
+        store,
+        out_shape=(shape, shape),
+        in_specs=[vmem] * 2,
+        out_specs=(hbm, hbm),
+        scratch_shapes=[dma((2,))],
+        compiler_params=pltpu.CompilerParams(vmem_limit_bytes=1024 * 1024),
+    )(pltpu.with_memory_space_constraint(x, pltpu.VMEM), pltpu.with_memory_space_constraint(r, pltpu.VMEM))
     return x.reshape(right_side.shape), r.reshape(right_side.shape)
 
 

time: 29.8 us -> 26.9 us (0.903)
  local copies, waits for them, and re-layouts: 2.22 us -> 0 us
  Pallas kernels: 26.8 us -> 26.1 us
    unnamed x4 -> x0, local copies, waits for them, and re-layouts: 2.22 us -> none
    pallas_call x1, Pallas kernels: 26.8 us -> 25.4 us  [body(): pl.pallas_call(functools.partial(kernel, (n_sfc, n_grp, count, ghost, pad...]
    pallas_call x0 -> x1, Pallas kernels: none -> 0.67 us  [body(): pl.pallas_call(store, out_shape=(shape, shape), in_specs=[vmem] * 2, out_...]
where the time goes in v2:
time: 26.9 us; the launch traced here: 26.7 us
  Pallas kernels  26.1 us (97%)
  between operations  0.64 us (2%)
    pallas_call x1, Pallas kernels, body(): pl.pallas_call(functools.partial(kernel, (n_sfc, n_grp, count, ghost, pad...  25.4 us
    pallas_call x1, Pallas kernels, body(): pl.pallas_call(store, out_shape=(shape, shape), in_specs=[vmem] * 2, out_...  0.67 us

profile of v2, /device:TPU:0, one launch (start us, length us, event | category | flops | bytes accessed | tf_op | source)
XLA Modules:
  0.0 26.7 jit_solution(9123658984736330291)
XLA Ops:
  0.6 25.4 %shard_map.149 = (f32[25,5,128]{2,1,0:T(8,128)S(1)}, f32[25,5,128]{2,1,0:T(8,128)S(1)}) custom-call(f32[25,5,128]{2,1,0:T(8,128)} %bitcast.4, s32[128]{0:T(128)} %level_hbm.1, s32[384]{0:T(512)} %own_hbm.1, s32[384]{0:T(512)} %near_hbm.1, s32[384]{0:T(512)} %kind_hbm.1, s32[384]{0:T(512)} %orient_hbm.1, f32[384]{0:T(512)} %pen_hbm.1, s32[384]{0:T(512)} %send_hbm.1, ...), custom_call_target="tpu_custom_call" | custom-call | tf_op jit(solution)/shard_map/pallas_call | solution.py:453
  26.1 0.7 %shard_map.150 = (f32[25,5,128]{2,1,0:T(8,128)}, f32[25,5,128]{2,1,0:T(8,128)}) custom-call(f32[25,5,128]{2,1,0:T(8,128)S(1)} %get-tuple-element.6.x_ref, f32[25,5,128]{2,1,0:T(8,128)S(1)} %get-tuple-element.7.r_ref), custom_call_target="tpu_custom_call" | custom-call | tf_op jit(solution)/shard_map/pallas_call | solution.py:481

commit v3 on v2

--- a/solution.py
+++ b/solution.py
@@ -14,6 +14,7 @@
 FACES = 6 * ROWS
 CUBE = 208
 ITERS = 3
+REACH = 4
 MOMENTS = 2 * ITERS
 MESSAGE = 56
 UNIT = 2.0**-12
@@ -143,7 +144,7 @@
     total = n_sfc * n_grp
     levels = ring_levels(total)
     slots_refs = rest[: len(levels)]
-    insem, xsend, xrecv, asend, arecv = rest[len(levels):]
+    insem, xsend, xrecv, asend, arecv, *relay = rest[len(levels):]
     me = lax.axis_index("sfc") * n_grp + lax.axis_index("grp")
     slots = 6 * count
     entries = 4 * ghost
@@ -163,7 +164,8 @@
     exists = [(me + offset >= 0) & (me + offset < total) for offset in OFFSETS]
 
     def near_device(k):
-        return me + jnp.where(exists[k], OFFSETS[k], 0)
+        offset = OFFSETS[k]
+        return me + jnp.where(exists[k], offset, offset - total if offset > 0 else offset + total)
 
     digits = [lax.rem(me // stride, size) for stride, size in levels]
 
@@ -177,15 +179,34 @@
             action()
 
     barrier = pltpu.get_barrier_semaphore()
+    relayed = len(levels) == 1 and REACH << ITERS == total
     greeted = 0
-    for level, (_, size) in enumerate(levels):
-        for step in range(1, size):
-            pl.semaphore_signal(barrier, inc=1, device_id=peer(level, step), device_id_type=LOGICAL)
-        greeted += size - 1
-    if len(levels) > 1:
+
+    def reach(distance, action):
+        for offset in (distance, -distance):
+            action(me + jnp.where((me + offset >= 0) & (me + offset < total), offset, offset - total if offset > 0 else offset + total))
+
+    if relayed:
+        for distance in range(1, REACH + 1):
+            reach(distance, lambda device: pl.semaphore_signal(barrier, inc=1, device_id=device, device_id_type=LOGICAL))
+        greeted = 2 * REACH
+    else:
+        for level, (_, size) in enumerate(levels):
+            for step in range(1, size):
+                pl.semaphore_signal(barrier, inc=1, device_id=peer(level, step), device_id_type=LOGICAL)
+            greeted += size - 1
         for k in range(4):
             pl.semaphore_signal(barrier, inc=1, device_id=near_device(k), device_id_type=LOGICAL)
         greeted += 4
+
+    def relay_send(turn_number):
+        if relayed:
+            reach(REACH << turn_number, lambda device: pl.semaphore_signal(
+                relay[turn_number], inc=1, device_id=device, device_id_type=LOGICAL))
+
+    def relay_wait(turn_number):
+        if relayed:
+            pl.semaphore_wait(relay[turn_number], 2)
 
     for k in range(4):
         @pl.when(jnp.logical_not(exists[k]))
@@ -274,6 +295,7 @@
         for k in (2, 3, 0, 1):
             guarded(k, copies[k].start)
         xcopies.append(copies)
+        relay_send(turn_number)
 
     send_out(0, raw)
 
@@ -351,6 +373,7 @@
             mine = mapped(turned(near_raw, near_codes, turn_table), near_kinds, forward)
         for k in range(4):
             guarded(k ^ 1, xcopies[it][k].wait_recv)
+        relay_wait(it)
         filler = jnp.zeros((ROWS - WIDTH, cols), F32)
         near_got = jnp.concatenate([xbuf[it, k ^ 1, :ROWS] for k in range(4)], axis=1)
         own_got = jnp.concatenate([xbuf[it, k, WIDTH : 2 * WIDTH] for k in range(4)], axis=1)
@@ -473,7 +496,8 @@
             dma((ITERS, 4)),
             dma((len(levels),)),
             dma((len(levels),)),
-        ],
+        ]
+        + [pltpu.SemaphoreType.REGULAR] * ITERS,
         compiler_params=pltpu.CompilerParams(
             collective_id=0, has_side_effects=True, vmem_limit_bytes=16 * 1024 * 1024
         ),

time: 26.9 us -> 26.6 us (0.989)
  Pallas kernels: 26.1 us -> 25.8 us
    pallas_call x1, Pallas kernels: 25.4 us -> 25.1 us  [body(): pl.pallas_call(functools.partial(kernel, (n_sfc, n_grp, count, ghost, pad...]
where the time goes in v3:
time: 26.6 us; the launch traced here: 26.4 us
  Pallas kernels  25.8 us (97%)
  between operations  0.64 us (2%)
    pallas_call x1, Pallas kernels, body(): pl.pallas_call(functools.partial(kernel, (n_sfc, n_grp, count, ghost, pad...  25.1 us
    pallas_call x1, Pallas kernels, body(): pl.pallas_call(store, out_shape=(shape, shape), in_specs=[vmem] * 2, out_...  0.67 us

profile of v3, /device:TPU:0, one launch (start us, length us, event | category | flops | bytes accessed | tf_op | source)
XLA Modules:
  0.0 26.4 jit_solution(12668498873780936303)
XLA Ops:
  0.6 25.1 %shard_map.149 = (f32[25,5,128]{2,1,0:T(8,128)S(1)}, f32[25,5,128]{2,1,0:T(8,128)S(1)}) custom-call(f32[25,5,128]{2,1,0:T(8,128)} %bitcast.4, s32[128]{0:T(128)} %level_hbm.1, s32[384]{0:T(512)} %own_hbm.1, s32[384]{0:T(512)} %near_hbm.1, s32[384]{0:T(512)} %kind_hbm.1, s32[384]{0:T(512)} %orient_hbm.1, f32[384]{0:T(512)} %pen_hbm.1, s32[384]{0:T(512)} %send_hbm.1, ...), custom_call_target="tpu_custom_call" | custom-call | tf_op jit(solution)/shard_map/pallas_call | solution.py:476
  25.8 0.7 %shard_map.150 = (f32[25,5,128]{2,1,0:T(8,128)}, f32[25,5,128]{2,1,0:T(8,128)}) custom-call(f32[25,5,128]{2,1,0:T(8,128)S(1)} %get-tuple-element.6.x_ref, f32[25,5,128]{2,1,0:T(8,128)S(1)} %get-tuple-element.7.r_ref), custom_call_target="tpu_custom_call" | custom-call | tf_op jit(solution)/shard_map/pallas_call | solution.py:505

commit v4 on v3

--- a/solution.py
+++ b/solution.py
@@ -301,9 +301,10 @@
 
     for name in ("turn", "mass", "maps", "vol", "lift"):
         loads[name].wait()
-    for f in range(6):
-        marks[f] = jnp.broadcast_to(jnp.where(face == f, 1.0, 0.0), (16, 2 * cols)).astype(BF16)
-    cells_t[...] = chosen.T.astype(BF16)
+    for pair in range(3):
+        marks[pair] = jnp.broadcast_to(jnp.where(face >> 1 == pair, 1.0, 0.0), (16, 2 * cols)).astype(BF16)
+    for end in range(2):
+        cells_t[:, end * count : (end + 1) * count] = jnp.where(face & 1 == end, chosen, 0.0).T.astype(BF16)
     mapz[...] = jnp.zeros_like(mapz)
     for s in range(4):
         mapz[s * ROWS : s * ROWS + WIDTH, 0:WIDTH] = maps_ref[:, s, :]
@@ -369,6 +370,8 @@
         first = FACES if last else 0
         image = image_of(state[first:], field_high, field_low, first)
         near_raw, own_raw = raw[:, :cols], raw[:, cols:]
+        if last:
+            moments.append(jnp.sum(field * image, axis=0, keepdims=True))
         if it:
             mine = mapped(turned(near_raw, near_codes, turn_table), near_kinds, forward)
         for k in range(4):
@@ -391,7 +394,9 @@
         jump = own_raw - theirs
         own_flux = diag[:, cols:] * jump
         if last:
-            moments.append(sum_all(field * image) + sum_all(own_flux * jump))
+            across = jnp.sum(own_flux * jump, axis=0, keepdims=True)
+            across = sum(across[:, i : i + count] for i in range(0, cols, count)) if cols % count == 0 else sum_all(across)
+            moments.append(jnp.sum(moments.pop() + across, axis=1, keepdims=True))
             lane_row = lax.broadcasted_iota(jnp.int32, (1, 128), 1)
             row = jnp.zeros((1, 128), F32)
             for i, part in enumerate(moments):
@@ -403,11 +408,14 @@
         flux = jnp.concatenate([near_flux, own_flux], axis=1)
         parts = []
         for part in split(flux):
-            for f in range(6):
+            for pair in range(3):
                 for half in range(ROWS // 16):
-                    parts.append(part[half * 16 : (half + 1) * 16] * marks[f])
-        faces = dot(jnp.concatenate(parts, axis=0), cells_t[...])
-        faces = faces[:FACES] + faces[FACES:]
+                    parts.append(part[half * 16 : (half + 1) * 16] * marks[pair])
+        sums = dot(jnp.concatenate(parts, axis=0), cells_t[...])
+        sums = sums[: FACES // 2] + sums[FACES // 2 :]
+        faces = jnp.concatenate(
+            [sums[f // 2 * ROWS : (f // 2 + 1) * ROWS, f % 2 * count : (f % 2 + 1) * count] for f in range(6)], axis=0
+        )
         both = dot(lift_ref[first:], jnp.concatenate(split(faces), axis=1))
         new = image + both[:, :count] + both[:, count:]
         if last:
@@ -481,8 +489,8 @@
         scratch_shapes=[pltpu.VMEM(operand.shape, operand.dtype) for operand in operands]
         + [
             pltpu.VMEM((2 * count, 8 * pad), BF16),
-            pltpu.VMEM((8 * pad, count), BF16),
-            pltpu.VMEM((6, 16, 8 * pad), BF16),
+            pltpu.VMEM((8 * pad, 2 * count), BF16),
+            pltpu.VMEM((3, 16, 8 * pad), BF16),
             pltpu.VMEM((4 * ROWS, 128), F32),
             pltpu.VMEM((ROWS, 8 * pad), F32),
             pltpu.VMEM((ITERS, 4, MESSAGE, pad), F32),

time: 26.6 us -> 26.2 us (0.985)
  Pallas kernels: 25.8 us -> 25.4 us
    pallas_call x1, Pallas kernels: 25.1 us -> 24.7 us  [body(): pl.pallas_call(functools.partial(kernel, (n_sfc, n_grp, count, ghost, pad...]
where the time goes in v4:
time: 26.2 us; the launch traced here: 26 us
  Pallas kernels  25.4 us (97%)
  between operations  0.64 us (2%)
    pallas_call x1, Pallas kernels, body(): pl.pallas_call(functools.partial(kernel, (n_sfc, n_grp, count, ghost, pad...  24.7 us
    pallas_call x1, Pallas kernels, body(): pl.pallas_call(store, out_shape=(shape, shape), in_specs=[vmem] * 2, out_...  0.67 us

profile of v4, /device:TPU:0, one launch (start us, length us, event | category | flops | bytes accessed | tf_op | source)
XLA Modules:
  0.0 26.0 jit_solution(1724587128755167049)
XLA Ops:
  0.6 24.7 %shard_map.149 = (f32[25,5,128]{2,1,0:T(8,128)S(1)}, f32[25,5,128]{2,1,0:T(8,128)S(1)}) custom-call(f32[25,5,128]{2,1,0:T(8,128)} %bitcast.4, s32[128]{0:T(128)} %level_hbm.1, s32[384]{0:T(512)} %own_hbm.1, s32[384]{0:T(512)} %near_hbm.1, s32[384]{0:T(512)} %kind_hbm.1, s32[384]{0:T(512)} %orient_hbm.1, f32[384]{0:T(512)} %pen_hbm.1, s32[384]{0:T(512)} %send_hbm.1, ...), custom_call_target="tpu_custom_call" | custom-call | tf_op jit(solution)/shard_map/pallas_call | solution.py:484
  25.4 0.7 %shard_map.150 = (f32[25,5,128]{2,1,0:T(8,128)}, f32[25,5,128]{2,1,0:T(8,128)}) custom-call(f32[25,5,128]{2,1,0:T(8,128)S(1)} %get-tuple-element.6.x_ref, f32[25,5,128]{2,1,0:T(8,128)S(1)} %get-tuple-element.7.r_ref), custom_call_target="tpu_custom_call" | custom-call | tf_op jit(solution)/shard_map/pallas_call | solution.py:513

commit v5 on v4

--- a/solution.py
+++ b/solution.py
@@ -55,15 +55,6 @@
     low = (volume - high.astype(np.float64)).astype(jnp.bfloat16)
     volume = np.concatenate([high, low])
     lift = both @ select.T
-    turn = np.zeros((8, ROWS, ROWS))
-    for code in range(8):
-        order = np.arange(WIDTH).reshape(5, 5)
-        order = order[::-1] if code & 1 else order
-        order = order[:, ::-1] if code & 2 else order
-        order = order.T if code & 4 else order
-        turn[code, np.arange(WIDTH), order.reshape(-1)] = 1.0
-    back = np.swapaxes(turn, 1, 2)
-    turns = np.concatenate([np.concatenate([m, m], axis=2).reshape(8 * ROWS, 2 * ROWS) for m in (turn, back)])
     face_mass = np.zeros((ROWS, 128))
     face_mass[:WIDTH] = UNIT * np.outer(w, w).reshape(-1, 1)
     cube_mass = np.zeros((CUBE, 128))
@@ -71,7 +62,6 @@
     bf = lambda a: jnp.asarray(np.asarray(a, np.float32), BF16)
     return (
         bf(select),
-        bf(turns),
         jnp.asarray(np.concatenate([face_mass, both @ cube_mass]), F32),
         bf(volume),
         bf(lift),
@@ -134,10 +124,10 @@
 def kernel(
     dims,
     rhs_hbm, level_hbm, own_hbm, near_hbm, kind_hbm, orient_hbm, pen_hbm, send_hbm, maps_hbm,
-    sel_hbm, turn_hbm, mass_hbm, vol_hbm, lift_hbm,
+    sel_hbm, mass_hbm, vol_hbm, lift_hbm,
     x_out, r_out,
     rhs_ref, level_ref, own_ref, near_ref, kind_ref, orient_ref, pen_ref, send_ref, maps_ref,
-    sel_ref, turn_ref, mass_ref, vol_ref, lift_ref,
+    sel_ref, mass_ref, vol_ref, lift_ref,
     cells, cells_t, marks, mapz, diag, xsrc, xbuf, asrc, *rest,
 ):
     n_sfc, n_grp, count, ghost, pad = dims
@@ -155,7 +145,7 @@
         ("near", near_hbm, near_ref), ("own", own_hbm, own_ref), ("send", send_hbm, send_ref),
         ("level", level_hbm, level_ref), ("rhs", rhs_hbm, rhs_ref), ("sel", sel_hbm, sel_ref),
         ("kind", kind_hbm, kind_ref), ("orient", orient_hbm, orient_ref), ("pen", pen_hbm, pen_ref),
-        ("turn", turn_hbm, turn_ref), ("mass", mass_hbm, mass_ref), ("maps", maps_hbm, maps_ref),
+        ("mass", mass_hbm, mass_ref), ("maps", maps_hbm, maps_ref),
         ("vol", vol_hbm, vol_ref), ("lift", lift_hbm, lift_ref),
     ]):
         loads[name] = pltpu.make_async_copy(src, dst, insem.at[i])
@@ -299,7 +289,7 @@
 
     send_out(0, raw)
 
-    for name in ("turn", "mass", "maps", "vol", "lift"):
+    for name in ("mass", "maps", "vol", "lift"):
         loads[name].wait()
     for pair in range(3):
         marks[pair] = jnp.broadcast_to(jnp.where(face >> 1 == pair, 1.0, 0.0), (16, 2 * cols)).astype(BF16)
@@ -322,12 +312,23 @@
     diag[:, cols:] = face_mass * strength
     mass_scale = mass_ref[ROWS:] * (scale * scale * scale)
 
-    def turned(values, codes, table):
-        forms = dot(table, jnp.concatenate(split(values), axis=0))
-        result = forms[:ROWS]
-        for code in range(1, 8):
-            result = jnp.where(codes == code, forms[code * ROWS : (code + 1) * ROWS], result)
-        return result
+    grid = [[row * NODES + column for column in range(NODES)] for row in range(NODES)]
+    orders = [
+        [n for row in grid[::-1] for n in row],
+        [n for row in grid for n in row[::-1]],
+        [n for column in zip(*grid) for n in column],
+    ]
+
+    def turned(values, codes, forwards):
+        rest = jnp.zeros((ROWS - WIDTH, values.shape[1]), F32)
+        for bit in (0, 1, 2) if forwards else (2, 1, 0):
+            if bit == 0:
+                moved = [values[g * NODES : (g + 1) * NODES] for g in range(NODES)[::-1]]
+            else:
+                moved = [values[n : n + 1] for n in orders[bit]]
+            moved = jnp.concatenate(moved + [rest], axis=0)
+            values = jnp.where((codes >> bit) & 1 == 1, moved, values)
+        return values
 
     def mapped(values, kinds, table):
         high, low = split(values)
@@ -337,8 +338,6 @@
             result = jnp.where(kinds == s + 2, forms[s * ROWS : (s + 1) * ROWS], result)
         return result
 
-    turn_table = turn_ref[: 8 * ROWS]
-    back_table = turn_ref[8 * ROWS :]
     own_kinds = ordered[2:3].astype(jnp.int32)
     own_codes = ordered[3:4].astype(jnp.int32)
 
@@ -373,7 +372,7 @@
         if last:
             moments.append(jnp.sum(field * image, axis=0, keepdims=True))
         if it:
-            mine = mapped(turned(near_raw, near_codes, turn_table), near_kinds, forward)
+            mine = mapped(turned(near_raw, near_codes, True), near_kinds, forward)
         for k in range(4):
             guarded(k ^ 1, xcopies[it][k].wait_recv)
         relay_wait(it)
@@ -389,8 +388,8 @@
             near_kinds = info[0].astype(jnp.int32)
             near_codes = info[1].astype(jnp.int32)
             diag[:, :cols] = face_mass * info[2]
-            mine = mapped(turned(near_raw, near_codes, turn_table), near_kinds, forward)
-        theirs = mapped(turned(near_got, own_codes, turn_table), own_kinds, forward)
+            mine = mapped(turned(near_raw, near_codes, True), near_kinds, forward)
+        theirs = mapped(turned(near_got, own_codes, True), own_kinds, forward)
         jump = own_raw - theirs
         own_flux = diag[:, cols:] * jump
         if last:
@@ -404,7 +403,7 @@
             asrc[0] = row
             level_start(0)
         near_flux = diag[:, :cols] * (mine - own_got)
-        near_flux = turned(mapped(near_flux, near_kinds, backward), near_codes, back_table)
+        near_flux = turned(mapped(near_flux, near_kinds, backward), near_codes, False)
         flux = jnp.concatenate([near_flux, own_flux], axis=1)
         parts = []
         for part in split(flux):

time: 26.2 us -> 25.4 us (0.969)
  Pallas kernels: 25.4 us -> 24.6 us
    pallas_call x1, Pallas kernels: 24.7 us -> 23.9 us  [body(): pl.pallas_call(functools.partial(kernel, (n_sfc, n_grp, count, ghost, pad...]
where the time goes in v5:
time: 25.4 us; the launch traced here: 25.2 us
  Pallas kernels  24.6 us (97%)
  between operations  0.64 us (3%)
    pallas_call x1, Pallas kernels, body(): pl.pallas_call(functools.partial(kernel, (n_sfc, n_grp, count, ghost, pad...  23.9 us
    pallas_call x1, Pallas kernels, body(): pl.pallas_call(store, out_shape=(shape, shape), in_specs=[vmem] * 2, out_...  0.67 us

profile of v5, /device:TPU:0, one launch (start us, length us, event | category | flops | bytes accessed | tf_op | source)
XLA Modules:
  0.0 25.2 jit_solution(10960923398756407610)
XLA Ops:
  0.6 23.9 %shard_map.140 = (f32[25,5,128]{2,1,0:T(8,128)S(1)}, f32[25,5,128]{2,1,0:T(8,128)S(1)}) custom-call(f32[25,5,128]{2,1,0:T(8,128)} %bitcast.4, s32[128]{0:T(128)} %level_hbm.1, s32[384]{0:T(512)} %own_hbm.1, s32[384]{0:T(512)} %near_hbm.1, s32[384]{0:T(512)} %kind_hbm.1, s32[384]{0:T(512)} %orient_hbm.1, f32[384]{0:T(512)} %pen_hbm.1, s32[384]{0:T(512)} %send_hbm.1, ...), custom_call_target="tpu_custom_call" | custom-call | tf_op jit(solution)/shard_map/pallas_call | solution.py:483
  24.5 0.7 %shard_map.141 = (f32[25,5,128]{2,1,0:T(8,128)}, f32[25,5,128]{2,1,0:T(8,128)}) custom-call(f32[25,5,128]{2,1,0:T(8,128)S(1)} %get-tuple-element.6.x_ref, f32[25,5,128]{2,1,0:T(8,128)S(1)} %get-tuple-element.7.r_ref), custom_call_target="tpu_custom_call" | custom-call | tf_op jit(solution)/shard_map/pallas_call | solution.py:512

commit v6 on v5

--- a/solution.py
+++ b/solution.py
@@ -54,7 +54,6 @@
     high = volume.astype(jnp.bfloat16)
     low = (volume - high.astype(np.float64)).astype(jnp.bfloat16)
     volume = np.concatenate([high, low])
-    lift = both @ select.T
     face_mass = np.zeros((ROWS, 128))
     face_mass[:WIDTH] = UNIT * np.outer(w, w).reshape(-1, 1)
     cube_mass = np.zeros((CUBE, 128))
@@ -64,7 +63,6 @@
         bf(select),
         jnp.asarray(np.concatenate([face_mass, both @ cube_mass]), F32),
         bf(volume),
-        bf(lift),
     )
 
 
@@ -124,10 +122,10 @@
 def kernel(
     dims,
     rhs_hbm, level_hbm, own_hbm, near_hbm, kind_hbm, orient_hbm, pen_hbm, send_hbm, maps_hbm,
-    sel_hbm, mass_hbm, vol_hbm, lift_hbm,
+    sel_hbm, mass_hbm, vol_hbm,
     x_out, r_out,
     rhs_ref, level_ref, own_ref, near_ref, kind_ref, orient_ref, pen_ref, send_ref, maps_ref,
-    sel_ref, mass_ref, vol_ref, lift_ref,
+    sel_ref, mass_ref, vol_ref,
     cells, cells_t, marks, mapz, diag, xsrc, xbuf, asrc, *rest,
 ):
     n_sfc, n_grp, count, ghost, pad = dims
@@ -146,7 +144,7 @@
         ("level", level_hbm, level_ref), ("rhs", rhs_hbm, rhs_ref), ("sel", sel_hbm, sel_ref),
         ("kind", kind_hbm, kind_ref), ("orient", orient_hbm, orient_ref), ("pen", pen_hbm, pen_ref),
         ("mass", mass_hbm, mass_ref), ("maps", maps_hbm, maps_ref),
-        ("vol", vol_hbm, vol_ref), ("lift", lift_hbm, lift_ref),
+        ("vol", vol_hbm, vol_ref),
     ]):
         loads[name] = pltpu.make_async_copy(src, dst, insem.at[i])
         loads[name].start()
@@ -289,7 +287,7 @@
 
     send_out(0, raw)
 
-    for name in ("mass", "maps", "vol", "lift"):
+    for name in ("mass", "maps", "vol"):
         loads[name].wait()
     for pair in range(3):
         marks[pair] = jnp.broadcast_to(jnp.where(face >> 1 == pair, 1.0, 0.0), (16, 2 * cols)).astype(BF16)
@@ -362,12 +360,38 @@
 
     basis = [field]
     moments = [sum_all(field * field)]
-    state = jnp.concatenate([trace_high + trace_low, field], axis=0)
+
+    def blank(rows):
+        return jnp.zeros((rows, count), F32)
+
+    def lifted(faces):
+        part = [faces[f * ROWS : (f + 1) * ROWS] for f in range(6)]
+        lines = []
+        for a in range(NODES):
+            for b in range(NODES):
+                g = a * NODES + b
+                line = jnp.concatenate([part[4][g : g + 1], blank(3), part[5][g : g + 1], blank(3)], axis=0)
+                for f, here, at in ((0, a == 0, b), (1, a == 4, b), (2, b == 0, a), (3, b == 4, a)):
+                    if here:
+                        line = line + jnp.concatenate([part[f][at * NODES : (at + 1) * NODES], blank(8 - NODES)], axis=0)
+                lines.append(line)
+        return jnp.concatenate(lines + [blank(CUBE - WIDTH * 8)], axis=0)
+
+    def traces(v):
+        five = lambda a, b: v[(a * NODES + b) * 8 : (a * NODES + b) * 8 + NODES]
+        pieces = []
+        for a in (0, 4):
+            pieces += [five(a, b) for b in range(NODES)] + [blank(ROWS - WIDTH)]
+        for b in (0, 4):
+            pieces += [five(a, b) for a in range(NODES)] + [blank(ROWS - WIDTH)]
+        for c in (0, 4):
+            pieces += [v[g * 8 + c : g * 8 + c + 1] for g in range(WIDTH)] + [blank(ROWS - WIDTH)]
+        return jnp.concatenate(pieces, axis=0)
+
     mine = None
     for it in range(ITERS):
         last = it + 1 == ITERS
-        first = FACES if last else 0
-        image = image_of(state[first:], field_high, field_low, first)
+        image = image_of(basis[-1], field_high, field_low, FACES)
         near_raw, own_raw = raw[:, :cols], raw[:, cols:]
         if last:
             moments.append(jnp.sum(field * image, axis=0, keepdims=True))
@@ -415,17 +439,14 @@
         faces = jnp.concatenate(
             [sums[f // 2 * ROWS : (f // 2 + 1) * ROWS, f % 2 * count : (f % 2 + 1) * count] for f in range(6)], axis=0
         )
-        both = dot(lift_ref[first:], jnp.concatenate(split(faces), axis=1))
-        new = image + both[:, :count] + both[:, count:]
+        new = image + lifted(faces)
         if last:
             basis.append(new)
             break
-        state = new
-        trace = state[:FACES]
-        trace_high, trace_low = high_low(trace)
+        trace_high, trace_low = high_low(traces(new))
         raw = gather(trace_high, trace_low)
         send_out(it + 1, raw)
-        field = state[FACES:]
+        field = new
         field_high, field_low = split(field)
         moments.append(sum_all(basis[-1] * field))
         moments.append(sum_all(field * field))

time: 25.4 us -> 25.2 us (level)
  no operation moved by 1% of the time
where the time goes in v6:
time: 25.2 us; the launch traced here: 25 us
  Pallas kernels  24.4 us (97%)
  between operations  0.64 us (3%)
    pallas_call x1, Pallas kernels, body(): pl.pallas_call(functools.partial(kernel, (n_sfc, n_grp, count, ghost, pad...  23.7 us
    pallas_call x1, Pallas kernels, body(): pl.pallas_call(store, out_shape=(shape, shape), in_specs=[vmem] * 2, out_...  0.67 us

profile of v6, /device:TPU:0, one launch (start us, length us, event | category | flops | bytes accessed | tf_op | source)
XLA Modules:
  0.0 25.0 jit_solution(7354155107728608761)
XLA Ops:
  0.6 23.7 %shard_map.131 = (f32[25,5,128]{2,1,0:T(8,128)S(1)}, f32[25,5,128]{2,1,0:T(8,128)S(1)}) custom-call(f32[25,5,128]{2,1,0:T(8,128)} %bitcast.4, s32[128]{0:T(128)} %level_hbm.1, s32[384]{0:T(512)} %own_hbm.1, s32[384]{0:T(512)} %near_hbm.1, s32[384]{0:T(512)} %kind_hbm.1, s32[384]{0:T(512)} %orient_hbm.1, f32[384]{0:T(512)} %pen_hbm.1, s32[384]{0:T(512)} %send_hbm.1, ...), custom_call_target="tpu_custom_call" | custom-call | tf_op jit(solution)/shard_map/pallas_call | solution.py:504
  24.4 0.7 %shard_map.132 = (f32[25,5,128]{2,1,0:T(8,128)}, f32[25,5,128]{2,1,0:T(8,128)}) custom-call(f32[25,5,128]{2,1,0:T(8,128)S(1)} %get-tuple-element.6.x_ref, f32[25,5,128]{2,1,0:T(8,128)S(1)} %get-tuple-element.7.r_ref), custom_call_target="tpu_custom_call" | custom-call | tf_op jit(solution)/shard_map/pallas_call | solution.py:533
